TPU v7x, 32 devices: a whole 2x2x4 slice. The times are simulated.
32 devices in a mesh: dim: 8 (over y, x, core), batch: 4 (over z).
Axes of the slice: x: 2, y: 2, z: 4, core: 2. Of those that a mesh axis runs over, the one named last changes fastest.
Arguments:
- start: float32 [1024, 4096], P('batch', 'dim'), may hold values from -6 to 6
- increments: float32 [3, 1024, 4096], P(None, 'batch', 'dim'), may hold values from -0.75 to 0.75
- w_in: bfloat16 [4096, 4096], P(None, 'dim'), may hold values from -0.09375 to 0.09375
- w_out: bfloat16 [4096, 4096], P('dim'), may hold values from -0.09375 to 0.09375
- initial: float32 [], replicated, may hold values from 4 to 5.5
Outputs:
- residual: float32 [1024], P('batch')
- grad_in: float32 [4096, 4096], P('batch', 'dim')
- grad_out: float32 [4096, 4096], P('dim', 'batch')
All inputs are finite; a program needn't handle non-finite values.
Results may differ from a plain program's by a relative error of at most 0.0051.
Values may be sent and summed in bfloat16 or wider, within the bound.
No kernel may reach another device: no remote copies, remote signals or barrier semaphores. Data moves between devices by JAX's collectives and lax.ppermute only.
A program may use at most 128 MiB of HBM per device.

v0:
```python
import math
import jax
import jax.numpy as jnp
from jax import lax
from jax.sharding import PartitionSpec as P

D = 4096
STEPS = 3
time_step = 1.0 / 64.0
lam_coef = 50.0
noise_coef = math.sqrt(2.0)


def on_device(start, increments, w_in, w_out, initial):
    zscale = 2.0 / math.sqrt(D)
    state = start
    saved = []
    ysum = jnp.zeros((start.shape[0],), jnp.float32)
    out_cols = lax.all_to_all(w_out, "dim", split_axis=1, concat_axis=0, tiled=True)
    for step in range(STEPS):
        inc = increments[step]
        whole = lax.all_gather(state.astype(jnp.bfloat16), "dim", axis=1, tiled=True)
        hidden = jnp.dot(whole, w_in, preferred_element_type=jnp.float32)
        act = jax.nn.silu(hidden).astype(jnp.bfloat16)
        act_whole = lax.all_gather(act, "dim", axis=1, tiled=True)
        zval = zscale * jnp.dot(act_whole, out_cols, preferred_element_type=jnp.float32)
        inner = jnp.sum(zval * inc, 1)
        square = jnp.sum(zval * zval, 1)
        inner_all, square_all = lax.psum((inner, square), "dim")
        ysum = ysum + 0.5 * lam_coef * time_step * square_all + inner_all
        saved.append((whole, hidden, act, zval))
        state = state + noise_coef * inc
    norm_local = jnp.sum(state * state, 1)
    norm_sq = lax.psum(norm_local, "dim")
    residual = initial + ysum - jnp.log((1.0 + norm_sq) * 0.5)
    grad_in = jnp.zeros(w_in.shape, jnp.float32)
    grad_out = jnp.zeros(w_out.shape, jnp.float32)
    reduced_in = None
    reduced_out = None
    for step in range(STEPS):
        whole, hidden, act, zval = saved[step]
        gz = (zscale * residual[:, None] * (lam_coef * time_step * zval + increments[step])).astype(
            jnp.bfloat16
        )
        gz_whole = lax.all_gather(gz, "dim", axis=1, tiled=True)
        term_out = jnp.dot(act.T, gz_whole, preferred_element_type=jnp.float32)
        ga = jnp.dot(gz_whole, w_out.T, preferred_element_type=jnp.float32)
        sig = jax.nn.sigmoid(hidden)
        gh = (ga * sig * (1.0 + hidden * (1.0 - sig))).astype(jnp.bfloat16)
        term_in = jnp.dot(whole.T, gh, preferred_element_type=jnp.float32)
        grad_in = grad_in + term_in
        grad_out = grad_out + term_out
    reduced_in, reduced_out = (
        lax.psum_scatter(grad_in, "batch", scatter_dimension=0, tiled=True),
        lax.psum_scatter(grad_out, "batch", scatter_dimension=1, tiled=True),
    )
    return (residual, reduced_in, reduced_out)


def solution(mesh):
    return jax.shard_map(
        on_device,
        mesh=mesh,
        in_specs=(P("batch", "dim"), P(None, "batch", "dim"), P(None, "dim"), P("dim", None), P()),
        out_specs=(P("batch"), P("batch", "dim"), P("dim", "batch")),
        check_vma=False,
    )
```

profile of v0, /device:TPU:0, one launch (start us, length us, event | category | flops | bytes accessed | tf_op | source)
XLA Modules:
  0.0 635.2 jit_solution(16171568415561256104)
XLA Ops:
  7.2 0.0 all-gather.18.cloned.1.call-start
  7.2 2.6 fusion.35
  9.8 0.0 all-gather.18.cloned.1.call-update
  9.9 0.0 all-gather.14.cloned.1.call-start
  9.9 0.7 all-gather.14.cloned.1.call-update
  10.6 0.0 all-gather.10.cloned.1.call-start
  10.7 0.7 all-gather.10.cloned.1.call-update
  11.4 0.0 all-gather.20.cloned.1.call-start
  11.4 29.9 %all-gather.18.cloned.1.call-done = bf16[256,4096]{1,0:T(8,128)(2,1)} async-done(((bf16[256,512]{1,0:T(8,128)(2,1)}), bf16[256,4096]{1,0:T(8,128)(2,1)}) %all-gather.18.cloned.1.call-update) | async-done | bytes 2097168 | tf_op jit(solution)/shard_map/all_gather | solution.py:22
  41.3 4.9 multiply_convert_fusion
  46.1 0.0 all-gather.20.cloned.1.call-update
  46.2 0.0 all-gather.16.cloned.1.call-start
  46.2 25.6 %all-gather.14.cloned.1.call-done = bf16[256,4096]{1,0:T(8,128)(2,1)} async-done(((bf16[256,512]{1,0:T(8,128)(2,1)}), bf16[256,4096]{1,0:T(8,128)(2,1)}) %all-gather.14.cloned.1.call-update) | async-done | bytes 2097168 | tf_op jit(solution)/shard_map/all_gather | solution.py:22
  71.9 4.9 multiply_convert_fusion.1
  76.7 0.0 all-gather.16.cloned.1.call-update
  76.8 6.5 %copy.14 = bf16[512,4096]{0,1:T(8,128)(2,1)} copy(bf16[512,4096]{1,0:T(8,128)(2,1)} %param.8) | data formatting | bytes 8388608 | tf_op args[3]
  83.3 4.6 all-to-all-start
  87.9 0.0 all-gather.12.cloned.1.call-start
  87.9 19.7 %all-gather.10.cloned.1.call-done = bf16[256,4096]{1,0:T(8,128)(2,1)} async-done(((bf16[256,512]{1,0:T(8,128)(2,1)}), bf16[256,4096]{1,0:T(8,128)(2,1)}) %all-gather.10.cloned.1.call-update) | async-done | bytes 2097168 | tf_op jit(solution)/shard_map/all_gather | solution.py:22
  107.6 5.0 multiply_convert_fusion.2
  112.6 0.0 all-gather.12.cloned.1.call-update
  112.6 0.0 all-gather.22.cloned.1.call-start
  113.3 33.4 %all-to-all-done = bf16[512,8,512]{0,2,1:T(8,128)(2,1)} async-done(((bf16[512,8,512]{0,2,1:T(8,128)(2,1)}), bf16[512,8,512]{0,2,1:T(8,128)(2,1)}, u32[]{:S(2)}, u32[]{:S(2)}) %all-to-all-start) | async-done | bytes 4194336 | tf_op jit(solution)/shard_map/all_to_all | solution.py:19
  146.7 6.6 %copy.15 = bf16[8,512,512]{2,1,0:T(8,128)(2,1)} copy(bf16[8,512,512]{1,2,0:T(8,128)(2,1)} %bitcast.1) | data formatting | bytes 8388608 | tf_op jit(solution)/shard_map/all_to_all | solution.py:19
  153.3 0.0 all-gather.20.cloned.1.call-done
  153.3 4.1 fusion.41
  157.3 0.0 copy-start.4
  157.3 24.5 %all-gather.16.cloned.1.call-done = bf16[256,4096]{1,0:T(8,128)(2,1)} async-done(((bf16[256,512]{1,0:T(8,128)(2,1)}), bf16[256,4096]{1,0:T(8,128)(2,1)}) %all-gather.16.cloned.1.call-update) | async-done | bytes 2097168 | tf_op jit(solution)/shard_map/all_gather | solution.py:25
  181.8 4.9 fusion.40
  186.7 25.0 %all-gather.12.cloned.1.call-done = bf16[256,4096]{1,0:T(8,128)(2,1)} async-done(((bf16[256,512]{1,0:T(8,128)(2,1)}), bf16[256,4096]{1,0:T(8,128)(2,1)}) %all-gather.12.cloned.1.call-update) | async-done | bytes 2097168 | tf_op jit(solution)/shard_map/all_gather | solution.py:25
  211.7 0.0 copy-done.4
  211.7 5.3 fusion.19
  217.0 13.3 %all-reduce = (f32[256]{0:T(256)S(1)}, f32[256]{0:T(256)S(1)}, f32[256]{0:T(256)S(1)}, f32[256]{0:T(256)S(1)}, f32[256]{0:T(256)S(1)}, /*index=5*/f32[256]{0:T(256)S(1)}, f32[256]{0:T(256)S(1)}) all-reduce(f32[256]{0:T(256)S(1)} %get-tuple-element.13, f32[256]{0:T(256)S(1)} %get-tuple-element.14, ...), channel_id=1, replica_groups=mesh['dim'=8,'batch'=4] {'dim'}, use_global_device_ids=true, to_apply=%region_13.14 | all-reduce | flops 1792 | bytes 14336 | tf_op jit(solution)/shard_map/psum | solution.py:34
  230.3 0.6 broadcast_multiply_fusion
  230.9 2.4 fusion.14
  233.2 0.0 all-gather.22.cloned.1.call-update
  233.3 0.0 all-gather.24.cloned.1.call-start
  233.3 0.7 all-gather.24.cloned.1.call-update
  234.0 0.0 all-gather.26.cloned.1.call-start
  234.1 0.7 all-gather.26.cloned.1.call-update
  234.7 0.2 reduce-scatter.3.cloned.1.call-start
  235.0 26.5 %all-gather.22.cloned.1.call-done = bf16[256,4096]{1,0:T(8,128)(2,1)} async-done(((bf16[256,512]{1,0:T(8,128)(2,1)}), bf16[256,4096]{1,0:T(8,128)(2,1)}) %all-gather.22.cloned.1.call-update) | async-done | bytes 2097168 | tf_op jit(solution)/shard_map/all_gather | solution.py:45
  261.5 9.6 %fusion.8 = f32[512,4096]{1,0:T(8,128)} fusion(bf16[256,4096]{1,0:T(8,128)(2,1)} %all-gather.10.cloned.1.call-done, bf16[256,4096]{1,0:T(8,128)(2,1)} %all-gather.22.cloned.1.call-done, bf16[512,4096]{1,0:T(8,128)(2,1)} %param.8, f32[256,512]{1,0:T(8,128)} %get-tuple-element.35), kind=kOutput, calls=%fused_computation.13 | convolution fusion | flops 2148663296 | bytes 17301504 | tf_op jit(solution)/shard_map/dot_general | solution.py:50
  271.1 20.4 %all-gather.24.cloned.1.call-done = bf16[256,4096]{1,0:T(8,128)(2,1)} async-done(((bf16[256,512]{1,0:T(8,128)(2,1)}), bf16[256,4096]{1,0:T(8,128)(2,1)}) %all-gather.24.cloned.1.call-update) | async-done | bytes 2097168 | tf_op jit(solution)/shard_map/all_gather | solution.py:45
  291.5 0.0 copy-done.3
  291.5 8.7 %fusion.6 = f32[4096,512]{0,1:T(8,128)} fusion(bf16[256,4096]{1,0:T(8,128)(2,1)S(1)} %copy-done.3, bf16[256,4096]{1,0:T(8,128)(2,1)} %all-gather.24.cloned.1.call-done, bf16[512,4096]{1,0:T(8,128)(2,1)} %param.8, f32[256,512]{1,0:T(8,128)S(1)} %get-tuple-element.39), kind=kOutput, calls=%fused_computation.11 | convolution fusion | flops 2148663296 | bytes 17301504 | tf_op jit(solution)/shard_map/dot_general | solution.py:50
  300.2 21.4 %all-gather.26.cloned.1.call-done = bf16[256,4096]{1,0:T(8,128)(2,1)} async-done(((bf16[256,512]{1,0:T(8,128)(2,1)}), bf16[256,4096]{1,0:T(8,128)(2,1)}) %all-gather.26.cloned.1.call-update) | async-done | bytes 2097168 | tf_op jit(solution)/shard_map/all_gather | solution.py:45
  321.5 14.1 %fusion = f32[4096,512]{0,1:T(8,128)} fusion(f32[4096,512]{0,1:T(8,128)} %fusion.6, f32[512,4096]{1,0:T(8,128)} %fusion.8, bf16[256,4096]{1,0:T(8,128)(2,1)} %all-gather.18.cloned.1.call-done, bf16[256,4096]{1,0:T(8,128)(2,1)} %all-gather.26.cloned.1.call-done, bf16[512,4096]{1,0:T(8,128)(2,1)} %param.8, f32[256,512]{1,0:T(8,128)S(1)} %get-tuple-element.37), kind=kOutput, calls=%fused_computation.1 | convolution fusion | flops 2152857600 | bytes 34078720 | tf_op jit(solution)/shard_map/dot_general | solution.py:50
  335.6 0.0 reduce-scatter.3.cloned.1.call-update
  335.6 0.0 copy-start.6
  335.6 0.0 reduce-scatter.5.cloned.1.call-start
  335.7 1.5 copy-done
  337.2 0.0 copy-done.7
  337.2 1.3 fusion.42
  338.5 0.0 copy-done.6
  338.5 0.3 copy-done.1
  338.8 1.3 fusion.43
  340.1 0.3 copy-done.2
  340.4 0.0 copy-done.5
  340.4 4.6 add_add_fusion
  345.0 0.0 reduce-scatter.5.cloned.1.call-update
  345.0 135.4 %reduce-scatter.3.cloned.1.call-done = f32[1024,512]{0,1:T(8,128)} async-done(((f32[4096,512]{0,1:T(8,128)}), f32[1024,512]{0,1:T(8,128)}) %reduce-scatter.3.cloned.1.call-update) | async-done | bytes 2097168 | tf_op jit(solution)/shard_map/reduce_scatter | solution.py:54
  480.4 2.9 copy.18
  483.3 145.3 %reduce-scatter.5.cloned.1.call-done = f32[512,1024]{1,0:T(8,128)} async-done(((f32[512,4096]{1,0:T(8,128)}), f32[512,1024]{1,0:T(8,128)}) %reduce-scatter.5.cloned.1.call-update) | async-done | bytes 2097168 | tf_op jit(solution)/shard_map/reduce_scatter | solution.py:55
  (6 shorter events, 0.0 us)
Async XLA Ops:
  7.2 34.1 %all-gather.18.cloned.1.call-start = ((), (), s32[]{:S(2)}) async-start(), calls=%async_computation.7 | async-start | bytes 2359296 | tf_op jit(solution)/shard_map/all_gather | solution.py:22
  9.9 62.0 %all-gather.14.cloned.1.call-start = ((), (), s32[]{:S(2)}) async-start(), calls=%async_computation.5 | async-start | bytes 2359296 | tf_op jit(solution)/shard_map/all_gather | solution.py:22
  10.6 97.0 %all-gather.10.cloned.1.call-start = ((), (), s32[]{:S(2)}) async-start(), calls=%async_computation.3 | async-start | bytes 2359296 | tf_op jit(solution)/shard_map/all_gather | solution.py:22
  11.4 141.9 %all-gather.20.cloned.1.call-start = ((), (), s32[]{:S(2)}) async-start(), calls=%async_computation.8 | async-start | bytes 2359296 | tf_op jit(solution)/shard_map/all_gather | solution.py:25
  46.2 135.7 %all-gather.16.cloned.1.call-start = ((), (), s32[]{:S(2)}) async-start(), calls=%async_computation.6 | async-start | bytes 2359296 | tf_op jit(solution)/shard_map/all_gather | solution.py:25
  83.3 63.4 %all-to-all-start = ((bf16[512,8,512]{0,2,1:T(8,128)(2,1)}), bf16[512,8,512]{0,2,1:T(8,128)(2,1)}, u32[]{:S(2)}, u32[]{:S(2)}) async-start(bf16[512,8,512]{0,2,1:T(8,128)(2,1)} %bitcast.86), calls=%async_computation | async-start | bytes 8388608 | tf_op jit(solution)/shard_map/all_to_all | solution.py:19
  87.9 123.8 %all-gather.12.cloned.1.call-start = ((), (), s32[]{:S(2)}) async-start(), calls=%async_computation.4 | async-start | bytes 2359296 | tf_op jit(solution)/shard_map/all_gather | solution.py:25
  112.6 148.9 %all-gather.22.cloned.1.call-start = ((), (), s32[]{:S(2)}) async-start(), calls=%async_computation.9 | async-start | bytes 2359296 | tf_op jit(solution)/shard_map/all_gather | solution.py:45
  157.3 54.4 %copy-start.4 = (f32[3,256,512]{2,1,0:T(8,128)S(1)}, f32[3,256,512]{2,1,0:T(8,128)}, u32[]{:S(2)}) copy-start(f32[3,256,512]{2,1,0:T(8,128)} %param.6) | copy-start | bytes 4718596
  233.3 58.3 %all-gather.24.cloned.1.call-start = ((), (), s32[]{:S(2)}) async-start(), calls=%async_computation.10 | async-start | bytes 2359296 | tf_op jit(solution)/shard_map/all_gather | solution.py:45
  234.0 87.5 %all-gather.26.cloned.1.call-start = ((), (), s32[]{:S(2)}) async-start(), calls=%async_computation.11 | async-start | bytes 2359296 | tf_op jit(solution)/shard_map/all_gather | solution.py:45
  234.7 245.7 %reduce-scatter.3.cloned.1.call-start = ((), (), s32[]{:S(2)}) async-start(), calls=%async_computation.12 | async-start | bytes 10485760 | tf_op jit(solution)/shard_map/reduce_scatter | solution.py:54
  261.5 30.0 %copy-start.3 = (bf16[256,4096]{1,0:T(8,128)(2,1)S(1)}, bf16[256,4096]{1,0:T(8,128)(2,1)}, u32[]{:S(2)}) copy-start(bf16[256,4096]{1,0:T(8,128)(2,1)} %all-gather.14.cloned.1.call-done) | copy-start | bytes 6291460
  335.6 1.6 copy-start
  335.6 1.6 copy-start.7
  335.6 2.8 copy-start.6
  335.6 293.0 %reduce-scatter.5.cloned.1.call-start = ((), (), s32[]{:S(2)}) async-start(), calls=%async_computation.13 | async-start | bytes 10485760 | tf_op jit(solution)/shard_map/reduce_scatter | solution.py:55
  337.2 1.6 copy-start.1
  338.8 1.6 copy-start.2
  338.8 1.6 copy-start.5
Sparse Core Ops, SparseCore 0:
  10.4 30.8 all-gather.17
  43.7 28.0 all-gather.13
  73.7 33.8 all-gather.9
  109.3 43.5 all-gather.19
  154.6 27.1 all-gather.15
  183.6 28.0 all-gather.11
  233.4 28.0 all-gather.21
  263.4 28.0 all-gather.23
  293.4 28.0 all-gather.25
  335.8 144.6 reduce-scatter.2
  483.3 145.2 reduce-scatter.4
where the time goes:
time: 636 us; the launch traced here: 635 us
  waiting for transfers between devices  510 us (80%)
  matrix products  68.4 us (11%)
  local copies, waits for them, and re-layouts  18.1 us (3%)
  between operations  14.6 us (2%)
  blocking collectives  13.3 us (2%)
    reduce_scatter x1, waiting for transfers between devices, on_device(): lax.psum_scatter(grad_out, 'batch', scatter_dimension=1, tiled=True)  145 us
    reduce_scatter x1, waiting for transfers between devices, on_device(): lax.psum_scatter(grad_in, 'batch', scatter_dimension=0, tiled=True)  135 us
    all_gather x3, waiting for transfers between devices, on_device(): lax.all_gather(state.astype(jnp.bfloat16), 'dim', axis=1, tiled=True)  75.2 us
    all_gather x3, waiting for transfers between devices, on_device(): gz_whole = lax.all_gather(gz, 'dim', axis=1, tiled=True)  68.3 us
    all_gather x3, waiting for transfers between devices, on_device(): act_whole = lax.all_gather(act, 'dim', axis=1, tiled=True)  49.5 us
    all_to_all x1, waiting for transfers between devices, on_device(): lax.all_to_all(w_out, 'dim', split_axis=1, concat_axis=0, tiled=True)  33.4 us
    dot_general x3, matrix products, on_device(): term_in = jnp.dot(whole.T, gh, preferred_element_type=jnp.float32)  32.3 us
    dot_general x3, matrix products, on_device(): hidden = jnp.dot(whole, w_in, preferred_element_type=jnp.float32)  14.7 us
  transfers between devices with their start and end apart: 12, of which 11 were waited for; matrix products, arithmetic and copies ran while one was open for 10% of the time, Pallas kernels for 0%

commit v1 on v0

--- a/solution.py
+++ b/solution.py
@@ -22,7 +22,14 @@
         whole = lax.all_gather(state.astype(jnp.bfloat16), "dim", axis=1, tiled=True)
         hidden = jnp.dot(whole, w_in, preferred_element_type=jnp.float32)
         act = jax.nn.silu(hidden).astype(jnp.bfloat16)
-        act_whole = lax.all_gather(act, "dim", axis=1, tiled=True)
+        ring = [act]
+        for hop in range(7):
+            ring.append(lax.ppermute(ring[-1], "dim", [(dev, (dev + 1) % 8) for dev in range(8)]))
+        act_whole = jnp.roll(
+            jnp.concatenate(ring[::-1], axis=1),
+            (lax.axis_index("dim") + 1) * ring[0].shape[1],
+            axis=1,
+        )
         zval = zscale * jnp.dot(act_whole, out_cols, preferred_element_type=jnp.float32)
         inner = jnp.sum(zval * inc, 1)
         square = jnp.sum(zval * zval, 1)

time: 636 us -> 611 us (0.961)
  waiting for transfers between devices: 510 us -> 482 us
  matrix products: 68.4 us -> 58.6 us
  local copies, waits for them, and re-layouts: 18.1 us -> 27.3 us
    all_gather x3 -> x0, waiting for transfers between devices: 49.5 us -> none  [on_device(): act_whole = lax.all_gather(act, 'dim', axis=1, tiled=True)]
    ppermute x0 -> x21, waiting for transfers between devices: none -> 42.8 us  [on_device(): lax.ppermute(ring[-1], 'dim', [(dev, (dev + 1) % 8) for dev in range(8)])]
    all_to_all x1, waiting for transfers between devices: 33.4 us -> 0.01 us  [on_device(): lax.all_to_all(w_out, 'dim', split_axis=1, concat_axis=0, tiled=True)]
    all_gather x3, waiting for transfers between devices: 75.2 us -> 88.4 us  [on_device(): lax.all_gather(state.astype(jnp.bfloat16), 'dim', axis=1, tiled=True)]
    dot_general x3, matrix products: 14.2 us -> 4.99 us  [on_device(): jnp.dot(act_whole, out_cols, preferred_element_type=jnp.float32)]
    unnamed x18 -> x67, local copies, waits for them, and re-layouts: 11.6 us -> 20.7 us
  transfers between devices with their start and end apart: 12 -> 30, of which waited for: 11 -> 24; matrix products, arithmetic and copies ran while one was open for 10% -> 11% of each run, Pallas kernels for 0% -> 0%
where the time goes in v1:
time: 611 us; the launch traced here: 610 us
  waiting for transfers between devices  482 us (79%)
  matrix products  58.6 us (10%)
  local copies, waits for them, and re-layouts  27.3 us (4%)
  between operations  15.3 us (3%)
  blocking collectives  12.8 us (2%)
  starting transfers between devices  8.91 us (1%)
    reduce_scatter x1, waiting for transfers between devices, on_device(): lax.psum_scatter(grad_out, 'batch', scatter_dimension=1, tiled=True)  145 us
    reduce_scatter x1, waiting for transfers between devices, on_device(): lax.psum_scatter(grad_in, 'batch', scatter_dimension=0, tiled=True)  135 us
    all_gather x3, waiting for transfers between devices, on_device(): lax.all_gather(state.astype(jnp.bfloat16), 'dim', axis=1, tiled=True)  88.4 us
    all_gather x3, waiting for transfers between devices, on_device(): gz_whole = lax.all_gather(gz, 'dim', axis=1, tiled=True)  67.3 us
    ppermute x21, waiting for transfers between devices, on_device(): lax.ppermute(ring[-1], 'dim', [(dev, (dev + 1) % 8) for dev in range(8)])  42.8 us
    dot_general x3, matrix products, on_device(): term_in = jnp.dot(whole.T, gh, preferred_element_type=jnp.float32)  32.5 us
    unnamed x67, local copies, waits for them, and re-layouts  20.7 us
    dot_general x3, matrix products, on_device(): hidden = jnp.dot(whole, w_in, preferred_element_type=jnp.float32)  13.9 us
  transfers between devices with their start and end apart: 30, of which 24 were waited for; matrix products, arithmetic and copies ran while one was open for 11% of the time, Pallas kernels for 0%

profile of v1, /device:TPU:0, one launch (start us, length us, event | category | flops | bytes accessed | tf_op | source)
XLA Modules:
  0.0 609.9 jit_solution(10079918021536520125)
XLA Ops:
  7.2 2.6 fusion.44
  9.9 0.7 all-gather.9.cloned.1.call-update
  10.7 0.7 all-gather.7.cloned.1.call-update
  11.4 6.5 %copy.14 = bf16[512,4096]{0,1:T(8,128)(2,1)} copy(bf16[512,4096]{1,0:T(8,128)(2,1)} %param.10) | data formatting | bytes 8388608 | tf_op args[3]
  17.9 5.2 all-to-all-start
  23.1 35.1 %all-gather.11.cloned.1.call-done = bf16[256,4096]{1,0:T(8,128)(2,1)} async-done(((bf16[256,512]{1,0:T(8,128)(2,1)}), bf16[256,4096]{1,0:T(8,128)(2,1)}) %all-gather.11.cloned.1.call-update) | async-done | bytes 2097168 | tf_op jit(solution)/shard_map/all_gather | solution.py:22
  58.2 4.1 multiply_convert_fusion
  62.4 0.3 collective-permute-start.14
  62.7 28.3 %all-gather.9.cloned.1.call-done = bf16[256,4096]{1,0:T(8,128)(2,1)} async-done(((bf16[256,512]{1,0:T(8,128)(2,1)}), bf16[256,4096]{1,0:T(8,128)(2,1)}) %all-gather.9.cloned.1.call-update) | async-done | bytes 2097168 | tf_op jit(solution)/shard_map/all_gather | solution.py:22
  90.9 4.9 multiply_convert_fusion.1
  96.1 25.0 %all-gather.7.cloned.1.call-done = bf16[256,4096]{1,0:T(8,128)(2,1)} async-done(((bf16[256,512]{1,0:T(8,128)(2,1)}), bf16[256,4096]{1,0:T(8,128)(2,1)}) %all-gather.7.cloned.1.call-update) | async-done | bytes 2097168 | tf_op jit(solution)/shard_map/all_gather | solution.py:22
  121.1 4.9 multiply_convert_fusion.2
  125.9 0.2 collective-permute-start
  126.2 1.3 collective-permute-start.15
  127.8 4.9 collective-permute-done
  132.6 0.7 copy-done.8
  133.3 2.1 collective-permute-done.15
  135.5 2.8 collective-permute-done.8
  138.3 2.8 collective-permute-done.1
  141.1 2.8 collective-permute-done.16
  143.9 2.8 collective-permute-done.9
  146.7 2.8 collective-permute-done.2
  149.5 2.8 collective-permute-done.17
  152.3 2.8 collective-permute-done.10
  155.1 2.8 collective-permute-done.3
  157.9 2.8 collective-permute-done.18
  160.7 2.9 collective-permute-done.11
  163.7 2.8 collective-permute-done.4
  166.5 2.8 collective-permute-done.19
  170.0 6.5 %copy.15 = bf16[8,512,512]{2,1,0:T(8,128)(2,1)} copy(bf16[8,512,512]{1,2,0:T(8,128)(2,1)} %bitcast.1) | data formatting | bytes 8388608 | tf_op jit(solution)/shard_map/all_to_all | solution.py:19
  176.5 0.7 collective-permute-start.13
  177.3 0.4 collective-permute-done.20
  177.7 1.0 constant_dynamic-update-slice_fusion.23
  178.7 1.0 constant_dynamic-update-slice_fusion.22
  179.7 1.0 constant_dynamic-update-slice_fusion.21
  180.7 1.0 constant_dynamic-update-slice_fusion.20
  181.8 1.6 collective-permute-done.13
  183.5 1.0 constant_dynamic-update-slice_fusion.14
  184.5 1.0 constant_dynamic-update-slice_fusion.13
  185.6 1.3 fusion.2
  187.0 1.3 fusion.5
  188.4 1.2 constant_dynamic-update-slice_fusion.6
  189.6 1.0 constant_dynamic-update-slice_fusion.5
  190.8 2.4 fusion.28
  193.2 12.8 %all-reduce = (f32[256]{0:T(256)S(1)}, f32[256]{0:T(256)S(1)}, f32[256]{0:T(256)S(1)}, f32[256]{0:T(256)S(1)}, f32[256]{0:T(256)S(1)}, /*index=5*/f32[256]{0:T(256)S(1)}, f32[256]{0:T(256)S(1)}) all-reduce(f32[256]{0:T(256)S(1)} %get-tuple-element.14, f32[256]{0:T(256)S(1)} %get-tuple-element.15, ...), channel_id=1, replica_groups=mesh['dim'=8,'batch'=4] {'dim'}, use_global_device_ids=true, to_apply=%region_13.15 | all-reduce | flops 1792 | bytes 14336 | tf_op jit(solution)/shard_map/psum | solution.py:41
  206.0 0.6 broadcast_multiply_fusion
  206.6 2.3 fusion.23
  209.0 0.5 all-gather.15.cloned.1.call-update
  209.6 0.5 all-gather.17.cloned.1.call-update
  210.3 26.0 %all-gather.13.cloned.1.call-done = bf16[256,4096]{1,0:T(8,128)(2,1)} async-done(((bf16[256,512]{1,0:T(8,128)(2,1)}), bf16[256,4096]{1,0:T(8,128)(2,1)}) %all-gather.13.cloned.1.call-update) | async-done | bytes 2097168 | tf_op jit(solution)/shard_map/all_gather | solution.py:52
  236.3 9.6 %fusion.17 = f32[512,4096]{1,0:T(8,128)} fusion(bf16[256,4096]{1,0:T(8,128)(2,1)} %all-gather.7.cloned.1.call-done, bf16[256,4096]{1,0:T(8,128)(2,1)} %all-gather.13.cloned.1.call-done, bf16[512,4096]{1,0:T(8,128)(2,1)} %param.10, f32[256,512]{1,0:T(8,128)} %get-tuple-element.36), kind=kOutput, calls=%fused_computation.25 | convolution fusion | flops 2148663296 | bytes 17301504 | tf_op jit(solution)/shard_map/dot_general | solution.py:57
  245.9 20.2 %all-gather.15.cloned.1.call-done = bf16[256,4096]{1,0:T(8,128)(2,1)} async-done(((bf16[256,512]{1,0:T(8,128)(2,1)}), bf16[256,4096]{1,0:T(8,128)(2,1)}) %all-gather.15.cloned.1.call-update) | async-done | bytes 2097168 | tf_op jit(solution)/shard_map/all_gather | solution.py:52
  266.2 8.8 %fusion.15 = f32[4096,512]{0,1:T(8,128)} fusion(bf16[256,4096]{1,0:T(8,128)(2,1)S(1)} %copy-done.3, bf16[256,4096]{1,0:T(8,128)(2,1)} %all-gather.15.cloned.1.call-done, bf16[512,4096]{1,0:T(8,128)(2,1)} %param.10, f32[256,512]{1,0:T(8,128)} %get-tuple-element.40), kind=kOutput, calls=%fused_computation.23 | convolution fusion | flops 2148663296 | bytes 17301504 | tf_op jit(solution)/shard_map/dot_general | solution.py:57
  274.9 21.1 %all-gather.17.cloned.1.call-done = bf16[256,4096]{1,0:T(8,128)(2,1)} async-done(((bf16[256,512]{1,0:T(8,128)(2,1)}), bf16[256,4096]{1,0:T(8,128)(2,1)}) %all-gather.17.cloned.1.call-update) | async-done | bytes 2097168 | tf_op jit(solution)/shard_map/all_gather | solution.py:52
  296.0 14.1 %fusion = f32[4096,512]{0,1:T(8,128)} fusion(f32[4096,512]{0,1:T(8,128)} %fusion.15, f32[512,4096]{1,0:T(8,128)} %fusion.17, bf16[256,4096]{1,0:T(8,128)(2,1)} %all-gather.11.cloned.1.call-done, bf16[256,4096]{1,0:T(8,128)(2,1)} %all-gather.17.cloned.1.call-done, bf16[512,4096]{1,0:T(8,128)(2,1)} %param.10, f32[256,512]{1,0:T(8,128)S(1)} %get-tuple-element.38), kind=kOutput, calls=%fused_computation.1 | convolution fusion | flops 2152857600 | bytes 34078720 | tf_op jit(solution)/shard_map/dot_general | solution.py:57
  310.2 1.5 copy-done
  311.7 1.3 fusion.55
  313.0 0.3 copy-done.1
  313.3 1.3 fusion.56
  314.6 0.3 copy-done.2
  314.9 4.7 add_add_fusion
  319.6 135.3 %reduce-scatter.3.cloned.1.call-done = f32[1024,512]{0,1:T(8,128)} async-done(((f32[4096,512]{0,1:T(8,128)}), f32[1024,512]{0,1:T(8,128)}) %reduce-scatter.3.cloned.1.call-update) | async-done | bytes 2097168 | tf_op jit(solution)/shard_map/reduce_scatter | solution.py:61
  454.9 2.9 copy.18
  457.8 145.3 %reduce-scatter.5.cloned.1.call-done = f32[512,1024]{1,0:T(8,128)} async-done(((f32[512,4096]{1,0:T(8,128)}), f32[512,1024]{1,0:T(8,128)}) %reduce-scatter.5.cloned.1.call-update) | async-done | bytes 2097168 | tf_op jit(solution)/shard_map/reduce_scatter | solution.py:62
  (91 shorter events, 1.7 us)
Async XLA Ops:
  7.2 51.1 %all-gather.11.cloned.1.call-start = ((), (), s32[]{:S(2)}) async-start(), calls=%async_computation.5 | async-start | bytes 2359296 | tf_op jit(solution)/shard_map/all_gather | solution.py:22
  9.9 81.1 %all-gather.9.cloned.1.call-start = ((), (), s32[]{:S(2)}) async-start(), calls=%async_computation.4 | async-start | bytes 2359296 | tf_op jit(solution)/shard_map/all_gather | solution.py:22
  10.6 110.5 %all-gather.7.cloned.1.call-start = ((), (), s32[]{:S(2)}) async-start(), calls=%async_computation.3 | async-start | bytes 2359296 | tf_op jit(solution)/shard_map/all_gather | solution.py:22
  17.9 152.1 %all-to-all-start = ((bf16[512,8,512]{0,2,1:T(8,128)(2,1)}), bf16[512,8,512]{0,2,1:T(8,128)(2,1)}, u32[]{:S(2)}, u32[]{:S(2)}) async-start(bf16[512,8,512]{0,2,1:T(8,128)(2,1)} %bitcast.83), calls=%async_computation | async-start | bytes 8388608 | tf_op jit(solution)/shard_map/all_to_all | solution.py:19
  23.1 213.2 %all-gather.13.cloned.1.call-start = ((), (), s32[]{:S(2)}) async-start(), calls=%async_computation.6 | async-start | bytes 2359296 | tf_op jit(solution)/shard_map/all_gather | solution.py:52
  62.4 63.8 %collective-permute-start.14 = (bf16[256,512]{1,0:T(8,128)(2,1)S(1)}, bf16[256,512]{1,0:T(8,128)(2,1)S(1)}, u32[]{:S(2)}, u32[]{:S(2)}) collective-permute-start(bf16[256,512]{1,0:T(8,128)(2,1)S(1)} %get-tuple-element.37), channel_id=1, source_target_pairs={{0,4},{4,8},{8,12},{12,16},{16,20},{20,24},{24,28},{28,0},{1,5},{5... | collective-permute-start | bytes 786440 | tf_op jit(solution)/shard_map/ppermute | solution.py:27
  95.8 31.7 %collective-permute-start.7 = (bf16[256,512]{1,0:T(8,128)(2,1)S(1)}, bf16[256,512]{1,0:T(8,128)(2,1)S(1)}, u32[]{:S(2)}, u32[]{:S(2)}) collective-permute-start(bf16[256,512]{1,0:T(8,128)(2,1)S(1)} %get-tuple-element.39), channel_id=1, source_target_pairs={{0,4},{4,8},{8,12},{12,16},{16,20},{20,24},{24,28},{28,0},{1,5},{5... | collective-permute-start | bytes 786440 | tf_op jit(solution)/shard_map/ppermute | solution.py:27
  125.9 6.7 %collective-permute-start = (bf16[256,512]{1,0:T(8,128)(2,1)S(1)}, bf16[256,512]{1,0:T(8,128)(2,1)S(1)}, u32[]{:S(2)}, u32[]{:S(2)}) collective-permute-start(bf16[256,512]{1,0:T(8,128)(2,1)S(1)} %get-tuple-element.35), channel_id=1, source_target_pairs={{0,4},{4,8},{8,12},{12,16},{16,20},{20,24},{24,28},{28,0},{1,5},{5... | collective-permute-start | bytes 786440 | tf_op jit(solution)/shard_map/ppermute | solution.py:27
  126.2 9.3 %collective-permute-start.15 = (bf16[256,512]{1,0:T(8,128)(2,1)S(1)}, bf16[256,512]{1,0:T(8,128)(2,1)S(1)}, u32[]{:S(2)}, u32[]{:S(2)}) collective-permute-start(bf16[256,512]{1,0:T(8,128)(2,1)S(1)} %collective-permute-done.14), channel_id=1, source_target_pairs={{0,4},{4,8},{8,12},{12,16},{16,20},{20,24},{24,28},{28,0},{1,5},{5... | collective-permute-start | bytes 786440 | tf_op jit(solution)/shard_map/ppermute | solution.py:27
  127.5 10.7 %collective-permute-start.8 = (bf16[256,512]{1,0:T(8,128)(2,1)S(1)}, bf16[256,512]{1,0:T(8,128)(2,1)S(1)}, u32[]{:S(2)}, u32[]{:S(2)}) collective-permute-start(bf16[256,512]{1,0:T(8,128)(2,1)S(1)} %collective-permute-done.7), channel_id=1, source_target_pairs={{0,4},{4,8},{8,12},{12,16},{16,20},{20,24},{24,28},{28,0},{1,5},{5... | collective-permute-start | bytes 786440 | tf_op jit(solution)/shard_map/ppermute | solution.py:27
  132.6 0.7 copy-start.8
  133.3 7.7 %collective-permute-start.1 = (bf16[256,512]{1,0:T(8,128)(2,1)S(1)}, bf16[256,512]{1,0:T(8,128)(2,1)S(1)}, u32[]{:S(2)}, u32[]{:S(2)}) collective-permute-start(bf16[256,512]{1,0:T(8,128)(2,1)S(1)} %collective-permute-done), channel_id=1, source_target_pairs={{0,4},{4,8},{8,12},{12,16},{16,20},{20,24},{24,28},{28,0},{1,5},{5... | collective-permute-start | bytes 786440 | tf_op jit(solution)/shard_map/ppermute | solution.py:27
  135.5 8.4 %collective-permute-start.16 = (bf16[256,512]{1,0:T(8,128)(2,1)S(1)}, bf16[256,512]{1,0:T(8,128)(2,1)S(1)}, u32[]{:S(2)}, u32[]{:S(2)}) collective-permute-start(bf16[256,512]{1,0:T(8,128)(2,1)S(1)} %collective-permute-done.15), channel_id=1, source_target_pairs={{0,4},{4,8},{8,12},{12,16},{16,20},{20,24},{24,28},{28,0},{1,5},{5... | collective-permute-start | bytes 786440 | tf_op jit(solution)/shard_map/ppermute | solution.py:27
  138.3 8.4 %collective-permute-start.9 = (bf16[256,512]{1,0:T(8,128)(2,1)S(1)}, bf16[256,512]{1,0:T(8,128)(2,1)S(1)}, u32[]{:S(2)}, u32[]{:S(2)}) collective-permute-start(bf16[256,512]{1,0:T(8,128)(2,1)S(1)} %collective-permute-done.8), channel_id=1, source_target_pairs={{0,4},{4,8},{8,12},{12,16},{16,20},{20,24},{24,28},{28,0},{1,5},{5... | collective-permute-start | bytes 786440 | tf_op jit(solution)/shard_map/ppermute | solution.py:27
  141.1 35.4 %copy-start.10 = (bf16[256,512]{1,0:T(8,128)(2,1)}, bf16[256,512]{1,0:T(8,128)(2,1)S(1)}, u32[]{:S(2)}) copy-start(bf16[256,512]{1,0:T(8,128)(2,1)S(1)} %collective-permute-done.1) | copy-start | bytes 786436
  141.1 8.4 %collective-permute-start.2 = (bf16[256,512]{1,0:T(8,128)(2,1)S(1)}, bf16[256,512]{1,0:T(8,128)(2,1)S(1)}, u32[]{:S(2)}, u32[]{:S(2)}) collective-permute-start(bf16[256,512]{1,0:T(8,128)(2,1)S(1)} %collective-permute-done.1), channel_id=1, source_target_pairs={{0,4},{4,8},{8,12},{12,16},{16,20},{20,24},{24,28},{28,0},{1,5},{5... | collective-permute-start | bytes 786440 | tf_op jit(solution)/shard_map/ppermute | solution.py:27
  143.9 22.6 %copy-start.16 = (bf16[256,512]{1,0:T(8,128)(2,1)}, bf16[256,512]{1,0:T(8,128)(2,1)S(1)}, u32[]{:S(2)}) copy-start(bf16[256,512]{1,0:T(8,128)(2,1)S(1)} %collective-permute-done.16) | copy-start | bytes 786436
  143.9 8.4 %collective-permute-start.17 = (bf16[256,512]{1,0:T(8,128)(2,1)S(1)}, bf16[256,512]{1,0:T(8,128)(2,1)S(1)}, u32[]{:S(2)}, u32[]{:S(2)}) collective-permute-start(bf16[256,512]{1,0:T(8,128)(2,1)S(1)} %collective-permute-done.16), channel_id=1, source_target_pairs={{0,4},{4,8},{8,12},{12,16},{16,20},{20,24},{24,28},{28,0},{1,5},{5... | collective-permute-start | bytes 786440 | tf_op jit(solution)/shard_map/ppermute | solution.py:27
  146.7 8.4 %collective-permute-start.10 = (bf16[256,512]{1,0:T(8,128)(2,1)S(1)}, bf16[256,512]{1,0:T(8,128)(2,1)S(1)}, u32[]{:S(2)}, u32[]{:S(2)}) collective-permute-start(bf16[256,512]{1,0:T(8,128)(2,1)S(1)} %collective-permute-done.9), channel_id=1, source_target_pairs={{0,4},{4,8},{8,12},{12,16},{16,20},{20,24},{24,28},{28,0},{1,5},{5... | collective-permute-start | bytes 786440 | tf_op jit(solution)/shard_map/ppermute | solution.py:27
  149.5 27.0 %copy-start.12 = (bf16[256,512]{1,0:T(8,128)(2,1)}, bf16[256,512]{1,0:T(8,128)(2,1)S(1)}, u32[]{:S(2)}) copy-start(bf16[256,512]{1,0:T(8,128)(2,1)S(1)} %collective-permute-done.2) | copy-start | bytes 786436
  149.5 8.4 %collective-permute-start.3 = (bf16[256,512]{1,0:T(8,128)(2,1)S(1)}, bf16[256,512]{1,0:T(8,128)(2,1)S(1)}, u32[]{:S(2)}, u32[]{:S(2)}) collective-permute-start(bf16[256,512]{1,0:T(8,128)(2,1)S(1)} %collective-permute-done.2), channel_id=1, source_target_pairs={{0,4},{4,8},{8,12},{12,16},{16,20},{20,24},{24,28},{28,0},{1,5},{5... | collective-permute-start | bytes 786440 | tf_op jit(solution)/shard_map/ppermute | solution.py:27
  152.3 17.0 %copy-start.20 = (bf16[256,512]{1,0:T(8,128)(2,1)}, bf16[256,512]{1,0:T(8,128)(2,1)S(1)}, u32[]{:S(2)}) copy-start(bf16[256,512]{1,0:T(8,128)(2,1)S(1)} %collective-permute-done.17) | copy-start | bytes 786436
  152.3 8.4 %collective-permute-start.18 = (bf16[256,512]{1,0:T(8,128)(2,1)S(1)}, bf16[256,512]{1,0:T(8,128)(2,1)S(1)}, u32[]{:S(2)}, u32[]{:S(2)}) collective-permute-start(bf16[256,512]{1,0:T(8,128)(2,1)S(1)} %collective-permute-done.17), channel_id=1, source_target_pairs={{0,4},{4,8},{8,12},{12,16},{16,20},{20,24},{24,28},{28,0},{1,5},{5... | collective-permute-start | bytes 786440 | tf_op jit(solution)/shard_map/ppermute | solution.py:27
  155.1 11.3 %copy-start.18 = (bf16[256,512]{1,0:T(8,128)(2,1)}, bf16[256,512]{1,0:T(8,128)(2,1)S(1)}, u32[]{:S(2)}) copy-start(bf16[256,512]{1,0:T(8,128)(2,1)S(1)} %collective-permute-done.10) | copy-start | bytes 786436
  155.1 8.5 %collective-permute-start.11 = (bf16[256,512]{1,0:T(8,128)(2,1)S(1)}, bf16[256,512]{1,0:T(8,128)(2,1)}, u32[]{:S(2)}, u32[]{:S(2)}) collective-permute-start(bf16[256,512]{1,0:T(8,128)(2,1)S(1)} %collective-permute-done.10), channel_id=1, source_target_pairs={{0,4},{4,8},{8,12},{12,16},{16,20},{20,24},{24,28},{28,0},{1,5},{5... | collective-permute-start | bytes 786440 | tf_op jit(solution)/shard_map/ppermute | solution.py:27
  157.9 18.5 %copy-start.14 = (bf16[256,512]{1,0:T(8,128)(2,1)}, bf16[256,512]{1,0:T(8,128)(2,1)S(1)}, u32[]{:S(2)}) copy-start(bf16[256,512]{1,0:T(8,128)(2,1)S(1)} %collective-permute-done.3) | copy-start | bytes 786436
  157.9 8.5 %collective-permute-start.4 = (bf16[256,512]{1,0:T(8,128)(2,1)S(1)}, bf16[256,512]{1,0:T(8,128)(2,1)}, u32[]{:S(2)}, u32[]{:S(2)}) collective-permute-start(bf16[256,512]{1,0:T(8,128)(2,1)S(1)} %collective-permute-done.3), channel_id=1, source_target_pairs={{0,4},{4,8},{8,12},{12,16},{16,20},{20,24},{24,28},{28,0},{1,5},{5... | collective-permute-start | bytes 786440 | tf_op jit(solution)/shard_map/ppermute | solution.py:27
  160.7 8.5 %copy-start.21 = (bf16[256,512]{1,0:T(8,128)(2,1)}, bf16[256,512]{1,0:T(8,128)(2,1)S(1)}, u32[]{:S(2)}) copy-start(bf16[256,512]{1,0:T(8,128)(2,1)S(1)} %collective-permute-done.18) | copy-start | bytes 786436
  160.7 8.5 %collective-permute-start.19 = (bf16[256,512]{1,0:T(8,128)(2,1)S(1)}, bf16[256,512]{1,0:T(8,128)(2,1)}, u32[]{:S(2)}, u32[]{:S(2)}) collective-permute-start(bf16[256,512]{1,0:T(8,128)(2,1)S(1)} %collective-permute-done.18), channel_id=1, source_target_pairs={{0,4},{4,8},{8,12},{12,16},{16,20},{20,24},{24,28},{28,0},{1,5},{5... | collective-permute-start | bytes 786440 | tf_op jit(solution)/shard_map/ppermute | solution.py:27
  163.6 12.8 %collective-permute-start.12 = (bf16[256,512]{1,0:T(8,128)(2,1)}, bf16[256,512]{1,0:T(8,128)(2,1)}, u32[]{:S(2)}, u32[]{:S(2)}) collective-permute-start(bf16[256,512]{1,0:T(8,128)(2,1)} %collective-permute-done.11), channel_id=1, source_target_pairs={{0,4},{4,8},{8,12},{12,16},{16,20},{20,24},{24,28},{28,0},{1,5},{5... | collective-permute-start | bytes 786440 | tf_op jit(solution)/shard_map/ppermute | solution.py:27
  166.5 10.7 %collective-permute-start.5 = (bf16[256,512]{1,0:T(8,128)(2,1)}, bf16[256,512]{1,0:T(8,128)(2,1)}, u32[]{:S(2)}, u32[]{:S(2)}) collective-permute-start(bf16[256,512]{1,0:T(8,128)(2,1)} %collective-permute-done.4), channel_id=1, source_target_pairs={{0,4},{4,8},{8,12},{12,16},{16,20},{20,24},{24,28},{28,0},{1,5},{5... | collective-permute-start | bytes 786440 | tf_op jit(solution)/shard_map/ppermute | solution.py:27
  169.3 8.4 %collective-permute-start.20 = (bf16[256,512]{1,0:T(8,128)(2,1)}, bf16[256,512]{1,0:T(8,128)(2,1)}, u32[]{:S(2)}, u32[]{:S(2)}) collective-permute-start(bf16[256,512]{1,0:T(8,128)(2,1)} %collective-permute-done.19), channel_id=1, source_target_pairs={{0,4},{4,8},{8,12},{12,16},{16,20},{20,24},{24,28},{28,0},{1,5},{5... | collective-permute-start | bytes 786440 | tf_op jit(solution)/shard_map/ppermute | solution.py:27
  176.5 5.2 copy-start.17
  176.5 7.0 %collective-permute-start.13 = (bf16[256,512]{1,0:T(8,128)(2,1)}, bf16[256,512]{1,0:T(8,128)(2,1)S(1)}, u32[]{:S(2)}, u32[]{:S(2)}) collective-permute-start(bf16[256,512]{1,0:T(8,128)(2,1)} %collective-permute-done.12), channel_id=1, source_target_pairs={{0,4},{4,8},{8,12},{12,16},{16,20},{20,24},{24,28},{28,0},{1,5},{5... | collective-permute-start | bytes 786440 | tf_op jit(solution)/shard_map/ppermute | solution.py:27
  177.2 11.1 %collective-permute-start.6 = (bf16[256,512]{1,0:T(8,128)(2,1)}, bf16[256,512]{1,0:T(8,128)(2,1)S(1)}, u32[]{:S(2)}, u32[]{:S(2)}) collective-permute-start(bf16[256,512]{1,0:T(8,128)(2,1)} %collective-permute-done.5), channel_id=1, source_target_pairs={{0,4},{4,8},{8,12},{12,16},{16,20},{20,24},{24,28},{28,0},{1,5},{5... | collective-permute-start | bytes 786440 | tf_op jit(solution)/shard_map/ppermute | solution.py:27
  180.6 4.8 copy-start.19
  181.8 3.8 copy-start.5
  186.9 3.6 copy-start.15
  187.0 3.6 copy-start.13
  187.0 3.7 copy-start.11
  188.3 2.5 copy-start.6
  188.3 2.4 copy-start.9
  188.3 2.5 copy-start.4
  188.3 2.5 copy-start.7
  208.9 57.2 %all-gather.15.cloned.1.call-start = ((), (), s32[]{:S(2)}) async-start(), calls=%async_computation.7 | async-start | bytes 2359296 | tf_op jit(solution)/shard_map/all_gather | solution.py:52
  209.5 86.5 %all-gather.17.cloned.1.call-start = ((), (), s32[]{:S(2)}) async-start(), calls=%async_computation.8 | async-start | bytes 2359296 | tf_op jit(solution)/shard_map/all_gather | solution.py:52
  210.1 244.8 %reduce-scatter.3.cloned.1.call-start = ((), (), s32[]{:S(2)}) async-start(), calls=%async_computation.9 | async-start | bytes 10485760 | tf_op jit(solution)/shard_map/reduce_scatter | solution.py:61
  236.3 29.9 %copy-start.3 = (bf16[256,4096]{1,0:T(8,128)(2,1)S(1)}, bf16[256,4096]{1,0:T(8,128)(2,1)}, u32[]{:S(2)}) copy-start(bf16[256,4096]{1,0:T(8,128)(2,1)} %all-gather.9.cloned.1.call-done) | copy-start | bytes 6291460
  310.1 1.6 copy-start
  310.1 293.0 %reduce-scatter.5.cloned.1.call-start = ((), (), s32[]{:S(2)}) async-start(), calls=%async_computation.10 | async-start | bytes 10485760 | tf_op jit(solution)/shard_map/reduce_scatter | solution.py:62
  311.7 1.6 copy-start.1
  313.3 1.6 copy-start.2
Sparse Core Ops, SparseCore 0:
  10.4 47.7 all-gather.10
  60.7 30.2 all-gather.8
  92.8 28.2 all-gather.6
  209.0 27.1 all-gather.12
  238.0 28.0 all-gather.14
  267.9 28.0 all-gather.16
  310.3 144.6 reduce-scatter.2
  457.8 145.2 reduce-scatter.4
